TPU v7x, 256 devices: a whole 4x4x8 slice. The times are simulated.
256 devices in a mesh: slab: 64 (over z, x, core), rep: 4 (over y).
Axes of the slice: x: 4, y: 4, z: 8, core: 2. Of those that a mesh axis runs over, the one named last changes fastest.
Arguments:
- dipoles: float32 [24, 4096, 256], P('rep', 'slab'), parts along dimension 0, may hold values from -6 to 6
- inv_alpha: float32 [4096, 256], P('slab'), may hold values from 0.5 to 2
- row_site: int32 [2, 4096], P(None, 'slab'), may hold values from -1 to 63, as said below
- green: float32 [6, 128, 128, 512], P(None, None, 'slab'), may hold values from -6 to 6
Outputs:
- applied: float32 [24, 4096, 256], P('rep', 'slab'), parts along dimension 0
There are 4 independent parts, one for each index of `rep`. A program takes and returns all parts, laid end to end along the dimension named above; an argument that names none is the same for every part. Nothing has to cross between parts.
Inputs may be any that keep to these rules, and one draw needn't show every extreme that they name: `row_site`: slot r belongs to device r // 64 of slab. A live slot has y under 128 / 2 and z under 128 / 2; an empty slot has -1 in both entries. Live slots name distinct (y, z). Of one device's slots, at most 2 have z in any one block of 2 consecutive planes, and in every draw some block gets exactly 2 from every device.
All inputs are finite; a program needn't handle non-finite values.
Results may differ from a plain program's by a relative error of at most 0.00005.
Values sent between devices are 32-bit elements; how exact they have to be, the bound alone decides.
No kernel may reach another device: no remote copies, remote signals or barrier semaphores. Data moves between devices by JAX's collectives and lax.ppermute only.
A program may use at most 64 MiB of HBM per device.

v0:
```python
import math

import jax
import jax.numpy as jnp
from jax import lax
from jax.sharding import PartitionSpec as P

NX = 256
NY = 128
NZ = 128
CAP = 2


HIGH = lax.Precision.HIGHEST


def dft_table(count_in, length, count_out, direction_sign):
    index_in = jnp.arange(count_in)[:, None]
    index_out = jnp.arange(count_out)[None, :]
    phase_index = index_in * index_out % length
    angles = phase_index.astype(jnp.float32) * (2.0 * math.pi / length)
    cosine = jnp.cos(angles)
    sine_part = jnp.sin(angles) * direction_sign
    factor = 1.0 if direction_sign < 0 else 1.0 / length
    upper_rows = jnp.concatenate([cosine, sine_part], axis=1)
    lower_rows = jnp.concatenate([-sine_part, cosine], axis=1)
    return jnp.concatenate([upper_rows, lower_rows], axis=0) * factor


def middle_transform(values, count_in, length, count_out, direction_sign, pattern):
    index_out = jnp.arange(count_out)[:, None]
    index_in = jnp.arange(count_in)[None, :]
    angles = (index_out * index_in % length).astype(jnp.float32) * (2.0 * math.pi / length)
    factor = 1.0 if direction_sign < 0 else 1.0 / length
    cosine = jnp.cos(angles) * factor
    sine_part = jnp.sin(angles) * (direction_sign * factor)
    mixed_cos = jnp.einsum(pattern, cosine, values, precision=HIGH)
    mixed_sin = jnp.einsum(pattern, sine_part, values, precision=HIGH)
    half_width = values.shape[-1] // 2
    real_part = mixed_cos[..., :half_width] - mixed_sin[..., half_width:]
    imag_part = mixed_cos[..., half_width:] + mixed_sin[..., :half_width]
    return jnp.concatenate([real_part, imag_part], axis=-1)


def apply_kernel(spectrum, green):
    half_width = spectrum.shape[-1] // 2
    sym_index = ((0, 1, 2), (1, 3, 4), (2, 4, 5))
    results = []
    for vector in range(2):
        for target in range(3):
            total_re = jnp.zeros(spectrum.shape[1:-1] + (half_width,), jnp.float32)
            total_im = jnp.zeros(spectrum.shape[1:-1] + (half_width,), jnp.float32)
            for other in range(3):
                kernel = green[sym_index[target][other]]
                source = spectrum[vector * 3 + other]
                kern_re, kern_im = (kernel[..., :half_width], kernel[..., half_width:])
                src_re, src_im = (source[..., :half_width], source[..., half_width:])
                total_re = total_re + kern_re * src_re - kern_im * src_im
                total_im = total_im + kern_re * src_im + kern_im * src_re
            results.append(jnp.concatenate([total_re, total_im], axis=-1))
    return jnp.stack(results, axis=0)


def body(dipoles, inv_alpha, row_site, green):
    devices = lax.axis_size("slab")
    row_len = dipoles.shape[2] // 2
    planes = NZ // 2 // devices
    half_y = NY // 2
    half_z = NZ // 2
    occupied = row_site[0] >= 0
    dest_dev = jnp.where(occupied, row_site[1] // planes, -1)
    local_pos = row_site[1] % planes * half_y + row_site[0]
    slots_all = devices * CAP
    owner_hot = (dest_dev[:, None] == jnp.arange(devices)[None, :]).astype(jnp.int32)
    earlier = jnp.cumsum(owner_hot, axis=0) - owner_hot
    slot_index = jnp.sum(earlier * owner_hot, axis=1)
    target = jnp.where(occupied, dest_dev * CAP + slot_index, -1)
    packer = target[None, :] == jnp.arange(slots_all)[:, None]
    pack_float = packer.astype(jnp.float32)
    send_rows = jnp.einsum("qr,vrx->vqx", pack_float, dipoles, precision=HIGH)
    send_pos = jnp.sum(jnp.where(packer, local_pos[None, :] + 1, 0), axis=1) - 1
    send_pos = send_pos.astype(jnp.float32)[None, :]
    recv_rows, recv_pos = (
        lax.all_to_all(send_rows, "slab", split_axis=1, concat_axis=1, tiled=True),
        lax.all_to_all(send_pos, "slab", split_axis=1, concat_axis=1, tiled=True),
    )
    table_x = dft_table(row_len, NX, NX, -1)
    spectral_rows = jnp.einsum("vqx,xk->vqk", recv_rows, table_x, precision=HIGH)
    plane_cells = planes * half_y
    placer = (recv_pos[0].astype(jnp.int32)[None, :] == jnp.arange(plane_cells)[:, None]).astype(
        jnp.float32
    )
    plane_grid = jnp.einsum("cq,vqk->vck", placer, spectral_rows, precision=HIGH)
    plane_grid = plane_grid.reshape(6, planes, half_y, 2 * NX)
    y_spectrum = middle_transform(plane_grid, half_y, NY, NY, -1, "ky,vzyx->vzkx")
    z_spectrum = middle_transform(
        lax.all_to_all(y_spectrum, "slab", split_axis=2, concat_axis=1, tiled=True),
        half_z,
        NZ,
        NZ,
        -1,
        "kz,vzyx->vkyx",
    )
    image = apply_kernel(z_spectrum, green)
    z_back = middle_transform(image, NZ, NZ, half_z, 1, "kz,vzyx->vkyx")
    fields = middle_transform(
        lax.all_to_all(z_back, "slab", split_axis=1, concat_axis=2, tiled=True),
        NY,
        NY,
        half_y,
        1,
        "ky,vzyx->vzkx",
    )
    flat_fields = fields.reshape(6, plane_cells, 2 * NX)
    picked = jnp.einsum("cq,vck->vqk", placer, flat_fields, precision=HIGH)
    table_back = dft_table(NX, NX, row_len, 1)
    back_rows = jnp.einsum("vqk,kx->vqx", picked, table_back, precision=HIGH)
    returned = jnp.einsum(
        "qr,vqx->vrx",
        pack_float,
        lax.all_to_all(back_rows, "slab", split_axis=1, concat_axis=1, tiled=True),
        precision=HIGH,
    )
    row_mask = occupied.astype(jnp.float32)[None, :, None]
    alpha_re = inv_alpha[:, :row_len]
    alpha_im = inv_alpha[:, row_len:]
    dip_re = dipoles[:, :, :row_len]
    dip_im = dipoles[:, :, row_len:]
    out_re = alpha_re * dip_re - alpha_im * dip_im - returned[:, :, :row_len]
    out_im = alpha_re * dip_im + alpha_im * dip_re - returned[:, :, row_len:]
    return jnp.concatenate([out_re, out_im], axis=-1) * row_mask


def solution(mesh):
    return jax.shard_map(
        body,
        mesh=mesh,
        in_specs=(
            P("rep", "slab", None),
            P("slab", None),
            P(None, "slab"),
            P(None, None, "slab", None),
        ),
        out_specs=P("rep", "slab", None),
        check_vma=False,
    )
```

profile of v0, /device:TPU:1, one launch (start us, length us, event | category | flops | bytes accessed | tf_op | source)
XLA Modules:
  0.0 234.6 jit_solution(11281930884019723754)
XLA Ops:
  2.8 13.0 %all-to-all-start.1 = ((f32[1,64,2]{2,0,1:T(1,128)}), f32[1,64,2]{2,0,1:T(1,128)S(1)}, u32[]{:S(2)}, u32[]{:S(2)}) async-start(f32[1,64,2]{2,0,1:T(1,128)} %bitcast.8), calls=%async_computation.1 | async-start | bytes 65536 | tf_op jit(solution)/shard_map/all_to_all | solution.py:85
  15.7 1.6 convolution_bitcast_fusion.9
  17.3 1.5 copy.46
  18.8 6.3 %all-to-all-done.1 = f32[1,64,2]{2,0,1:T(1,128)S(1)} async-done(((f32[1,64,2]{2,0,1:T(1,128)}), f32[1,64,2]{2,0,1:T(1,128)S(1)}, u32[]{:S(2)}, u32[]{:S(2)}) %all-to-all-start.1) | async-done | bytes 544 | tf_op jit(solution)/shard_map/all_to_all | solution.py:85
  25.1 5.3 %all-to-all-start = ((f32[6,128,256]{2,0,1:T(8,128)}), f32[6,128,256]{2,0,1:T(8,128)S(1)}, u32[]{:S(2)}, u32[]{:S(2)}) async-start(f32[6,128,256]{2,0,1:T(8,128)} %copy.46), calls=%async_computation | async-start | bytes 2097152 | tf_op jit(solution)/shard_map/all_to_all | solution.py:84
  31.7 26.9 %all-to-all-done = f32[6,128,256]{2,0,1:T(8,128)S(1)} async-done(((f32[6,128,256]{2,0,1:T(8,128)}), f32[6,128,256]{2,0,1:T(8,128)S(1)}, u32[]{:S(2)}, u32[]{:S(2)}) %all-to-all-start) | async-done | bytes 786464 | tf_op jit(solution)/shard_map/all_to_all | solution.py:84
  58.6 1.6 fusion.8
  60.9 2.7 %convolution_bitcast_fusion.4 = f32[6,1,128,512]{2,3,0,1:T(8,128)S(1)} fusion(f32[6,64,512]{2,1,0:T(8,128)S(1)} %convolution_bitcast_fusion.8), kind=kOutput, calls=%fused_computation.20 | convolution fusion | flops 302112768 | bytes 2359296 | tf_op jit(solution)/shard_map/ky,vzyx->vzkx/dot_general | solution.py:38
  63.5 2.7 %convolution_bitcast_fusion.5 = f32[6,1,128,512]{2,3,0,1:T(8,128)S(1)} fusion(f32[6,64,512]{2,1,0:T(8,128)S(1)} %convolution_bitcast_fusion.8), kind=kOutput, calls=%fused_computation.21 | convolution fusion | flops 302104576 | bytes 2359296 | tf_op jit(solution)/shard_map/ky,vzyx->vzkx/dot_general | solution.py:37
  66.5 2.9 %copy.49 = f32[6,1,128,512]{3,1,0,2:T(1,128)} copy(f32[6,1,128,512]{2,3,0,1:T(8,128)S(1)} %pad_maximum_fusion) | data formatting | bytes 3145728 | tf_op jit(solution)/shard_map/concatenate | solution.py:42
  69.4 6.9 %all-to-all-start.2 = ((f32[6,1,128,512]{3,1,0,2:T(1,128)}), f32[6,1,128,512]{3,1,0,2:T(1,128)}, u32[]{:S(2)}, u32[]{:S(2)}) async-start(f32[6,1,128,512]{3,1,0,2:T(1,128)} %copy.49), calls=%async_computation.2 | async-start | bytes 3145728 | tf_op jit(solution)/shard_map/all_to_all | solution.py:97
  76.3 2.1 fusion.150
  78.4 1.3 copy.77
  79.8 1.3 copy.79
  81.8 1.2 copy.75
  83.1 32.1 %all-to-all-done.2 = f32[6,1,128,512]{3,1,0,2:T(1,128)} async-done(((f32[6,1,128,512]{3,1,0,2:T(1,128)}), f32[6,1,128,512]{3,1,0,2:T(1,128)}, u32[]{:S(2)}, u32[]{:S(2)}) %all-to-all-start.2) | async-done | bytes 1572896 | tf_op jit(solution)/shard_map/all_to_all | solution.py:97
  115.1 1.7 copy.74
  116.8 6.1 %convolution_bitcast_fusion = f32[6,128,2,512]{1,3,2,0:T(8,128)S(1)} fusion(f32[6,64,2,512]{3,0,2,1:T(8,128)S(1)} %bitcast.172), kind=kOutput, calls=%fused_computation.10 | convolution fusion | flops 604102656 | bytes 4718592 | tf_op jit(solution)/shard_map/kz,vzyx->vkyx/dot_general | solution.py:38
  123.0 6.5 %convolution_bitcast_fusion.1 = f32[6,128,2,512]{1,3,2,0:T(8,128)S(1)} fusion(f32[6,64,2,512]{3,0,2,1:T(8,128)S(1)} %bitcast.173), kind=kOutput, calls=%fused_computation.11 | convolution fusion | flops 604094464 | bytes 4718592 | tf_op jit(solution)/shard_map/kz,vzyx->vkyx/dot_general | solution.py:37
  132.7 3.7 %convolution_bitcast_fusion.2 = f32[6,64,2,512]{3,1,2,0:T(8,128)S(1)} fusion(f32[6,128,2,512]{1,3,2,0:T(8,128)S(1)} %fusion.32), kind=kOutput, calls=%fused_computation.18 | convolution fusion | flops 604102656 | bytes 4718592 | tf_op jit(solution)/shard_map/kz,vzyx->vkyx/dot_general | solution.py:38
  136.4 3.7 %convolution_bitcast_fusion.3 = f32[6,64,2,512]{3,1,2,0:T(8,128)S(1)} fusion(f32[6,128,2,512]{1,3,2,0:T(8,128)S(1)} %fusion.32), kind=kOutput, calls=%fused_computation.19 | convolution fusion | flops 604102656 | bytes 4718592 | tf_op jit(solution)/shard_map/kz,vzyx->vkyx/dot_general | solution.py:37
  140.6 2.6 %copy.60 = f32[6,64,2,512]{3,2,0,1:T(2,128)} copy(f32[6,64,2,512]{3,1,2,0:T(8,128)S(1)} %pad_maximum_fusion.1) | data formatting | bytes 3145728 | tf_op jit(solution)/shard_map/concatenate | solution.py:42
  143.1 6.4 %all-to-all-start.3 = ((f32[6,64,2,512]{3,2,0,1:T(2,128)}), f32[6,64,2,512]{3,2,0,1:T(2,128)S(1)}, u32[]{:S(2)}, u32[]{:S(2)}) async-start(f32[6,64,2,512]{3,2,0,1:T(2,128)} %copy.60), calls=%async_computation.3 | async-start | bytes 3145728 | tf_op jit(solution)/shard_map/all_to_all | solution.py:107
  150.6 38.0 %all-to-all-done.3 = f32[6,64,2,512]{3,2,0,1:T(2,128)S(1)} async-done(((f32[6,64,2,512]{3,2,0,1:T(2,128)}), f32[6,64,2,512]{3,2,0,1:T(2,128)S(1)}, u32[]{:S(2)}, u32[]{:S(2)}) %all-to-all-start.3) | async-done | bytes 1572896 | tf_op jit(solution)/shard_map/all_to_all | solution.py:107
  189.1 1.1 reshape.76
  190.2 1.1 convolution_bitcast_fusion.6
  191.4 1.1 convolution_bitcast_fusion.7
  192.6 1.4 fusion.4
  194.0 2.6 %fusion = f32[6,128,256]{2,1,0:T(8,128)S(1)} fusion(f32[6,512,128]{2,1,0:T(8,128)S(1)} %fusion.4, f32[256,128]{1,0:T(8,128)S(1)} %get-tuple-element.34, f32[256,128]{1,0:T(8,128)S(1)} %fusion.57, f32[256,128]{1,0:T(8,128)S(1)} %get-tuple-element.33), kind=kOutput, calls=%fused_computation.16 | convolution fusion | flops 1208483840 | bytes 2752512 | tf_op jit(solution)/shard_map/vqk,kx->vqx/dot_general | solution.py:117
  196.7 1.5 copy.63
  198.1 6.5 %all-to-all-start.4 = ((f32[6,128,256]{2,0,1:T(8,128)}), f32[6,128,256]{2,0,1:T(8,128)S(1)}, u32[]{:S(2)}, u32[]{:S(2)}) async-start(f32[6,128,256]{2,0,1:T(8,128)} %copy.63), calls=%async_computation.4 | async-start | bytes 2097152 | tf_op jit(solution)/shard_map/all_to_all | solution.py:121
  204.7 28.1 %all-to-all-done.4 = f32[6,128,256]{2,0,1:T(8,128)S(1)} async-done(((f32[6,128,256]{2,0,1:T(8,128)}), f32[6,128,256]{2,0,1:T(8,128)S(1)}, u32[]{:S(2)}, u32[]{:S(2)}) %all-to-all-start.4) | async-done | bytes 786464 | tf_op jit(solution)/shard_map/all_to_all | solution.py:121
  (63 shorter events, 12.6 us)
Async XLA Ops:
  2.8 22.3 %all-to-all-start.1 = ((f32[1,64,2]{2,0,1:T(1,128)}), f32[1,64,2]{2,0,1:T(1,128)S(1)}, u32[]{:S(2)}, u32[]{:S(2)}) async-start(f32[1,64,2]{2,0,1:T(1,128)} %bitcast.8), calls=%async_computation.1 | async-start | bytes 65536 | tf_op jit(solution)/shard_map/all_to_all | solution.py:85
  25.1 33.5 %all-to-all-start = ((f32[6,128,256]{2,0,1:T(8,128)}), f32[6,128,256]{2,0,1:T(8,128)S(1)}, u32[]{:S(2)}, u32[]{:S(2)}) async-start(f32[6,128,256]{2,0,1:T(8,128)} %copy.46), calls=%async_computation | async-start | bytes 2097152 | tf_op jit(solution)/shard_map/all_to_all | solution.py:84
  69.4 6.9 %copy-start = (f32[6,128,2,512]{3,2,1,0:T(2,128)S(1)}, f32[6,128,2,512]{3,2,1,0:T(2,128)}, u32[]{:S(2)}) copy-start(f32[6,128,2,512]{3,2,1,0:T(2,128)} %param.7) | copy-start | bytes 9437188
  69.4 45.7 %all-to-all-start.2 = ((f32[6,1,128,512]{3,1,0,2:T(1,128)}), f32[6,1,128,512]{3,1,0,2:T(1,128)}, u32[]{:S(2)}, u32[]{:S(2)}) async-start(f32[6,1,128,512]{3,1,0,2:T(1,128)} %copy.49), calls=%async_computation.2 | async-start | bytes 3145728 | tf_op jit(solution)/shard_map/all_to_all | solution.py:97
  78.4 2.7 %copy-start.3 = (f32[1,128,2,512]{3,2,1,0:T(2,128)S(1)}, f32[1,128,2,512]{3,2,1,0:T(2,128)}, u32[]{:S(2)}) copy-start(f32[1,128,2,512]{3,2,1,0:T(2,128)} %get-tuple-element.15) | copy-start | bytes 1572868
  78.4 2.9 %copy-start.2 = (f32[1,128,2,512]{3,2,1,0:T(2,128)S(1)}, f32[1,128,2,512]{3,2,1,0:T(2,128)}, u32[]{:S(2)}) copy-start(f32[1,128,2,512]{3,2,1,0:T(2,128)} %get-tuple-element.19) | copy-start | bytes 1572868
  79.8 1.8 copy-start.1
  143.1 45.4 %all-to-all-start.3 = ((f32[6,64,2,512]{3,2,0,1:T(2,128)}), f32[6,64,2,512]{3,2,0,1:T(2,128)S(1)}, u32[]{:S(2)}, u32[]{:S(2)}) async-start(f32[6,64,2,512]{3,2,0,1:T(2,128)} %copy.60), calls=%async_computation.3 | async-start | bytes 3145728 | tf_op jit(solution)/shard_map/all_to_all | solution.py:107
  196.6 8.0 %copy-start.6 = (s32[2,64]{1,0:T(2,128)S(1)}, s32[2,64]{1,0:T(2,128)}, u32[]{:S(2)}) copy-start(s32[2,64]{1,0:T(2,128)} %param.6) | copy-start | bytes 1540
  196.7 8.0 %copy-start.5 = (f32[64,256]{1,0:T(8,128)S(1)}, f32[64,256]{1,0:T(8,128)}, u32[]{:S(2)}) copy-start(f32[64,256]{1,0:T(8,128)} %param.5) | copy-start | bytes 196612
  198.1 35.3 %copy-start.4 = (f32[6,64,256]{2,1,0:T(8,128)S(1)}, f32[6,64,256]{2,1,0:T(8,128)}, u32[]{:S(2)}) copy-start(f32[6,64,256]{2,1,0:T(8,128)} %param.4) | copy-start | bytes 1179652
  198.1 34.7 %all-to-all-start.4 = ((f32[6,128,256]{2,0,1:T(8,128)}), f32[6,128,256]{2,0,1:T(8,128)S(1)}, u32[]{:S(2)}, u32[]{:S(2)}) async-start(f32[6,128,256]{2,0,1:T(8,128)} %copy.63), calls=%async_computation.4 | async-start | bytes 2097152 | tf_op jit(solution)/shard_map/all_to_all | solution.py:121
where the time goes:
time: 238 us; the launch traced here: 235 us
  waiting for transfers between devices  131 us (55%)
  starting transfers between devices  38.1 us (16%)
  matrix products  36.1 us (15%)
  local copies, waits for them, and re-layouts  19.3 us (8%)
  other arithmetic  9.07 us (4%)
    all_to_all x1, waiting for transfers between devices, body(): lax.all_to_all(z_back, 'slab', split_axis=1, concat_axis=2, tiled=True)  38 us
    all_to_all x1, waiting for transfers between devices, body(): lax.all_to_all(y_spectrum, 'slab', split_axis=2, concat_axis=1, tiled=True)  32.1 us
    all_to_all x1, waiting for transfers between devices, body(): lax.all_to_all(back_rows, 'slab', split_axis=1, concat_axis=1, tiled=True)  28.1 us
    all_to_all x1, waiting for transfers between devices, body(): lax.all_to_all(send_rows, 'slab', split_axis=1, concat_axis=1, tiled=True)  26.9 us
    dot_general x4, matrix products, middle_transform(): mixed_cos = jnp.einsum(pattern, cosine, values, precision=HIGH)  14 us
    dot_general x4, matrix products, middle_transform(): mixed_sin = jnp.einsum(pattern, sine_part, values, precision=HIGH)  13.6 us
    all_to_all x1, starting transfers between devices, body(): lax.all_to_all(send_pos, 'slab', split_axis=1, concat_axis=1, tiled=True)  13 us
    all_to_all x1, starting transfers between devices, body(): lax.all_to_all(y_spectrum, 'slab', split_axis=2, concat_axis=1, tiled=True)  6.92 us
  transfers between devices with their start and end apart: 5, of which 5 were waited for; matrix products, arithmetic and copies ran while one was open for 5% of the time, Pallas kernels for 0%

commit v1 on v0

v1 whole, which is shorter than its diff:
```python
import math

import jax
import jax.numpy as jnp
import numpy as np
from jax import lax
from jax.experimental import pallas as pl
from jax.experimental.pallas import tpu as pltpu
from jax.sharding import PartitionSpec as P

NX = 256
NY = 128
NZ = 128
LX = 128
DEVICES = 64
BLOCKS = 32
INTERPRET = False

F32 = jnp.float32
BF16 = jnp.bfloat16


def split_table(table):
    high = np.asarray(table, np.float32).astype(BF16)
    low = (table - high.astype(np.float64)).astype(np.float32).astype(BF16)
    return high, low


def phases(rows, columns, length, sign):
    angles = 2.0 * math.pi * (np.outer(rows, columns) % length) / length
    return np.cos(angles), sign * np.sin(angles)


def tables():
    y = np.arange(NY // 2)
    ky = np.arange(NY)
    z = np.concatenate([np.arange(0, NZ // 2, 2), np.arange(1, NZ // 2, 2)])
    kz = np.arange(NZ)
    x = np.arange(LX)
    kx = np.arange(NX)
    cos, sin = phases(ky, y, NY, -1.0)
    y_high, y_low = split_table(np.concatenate([cos, sin]))
    y_forward = np.concatenate([y_high, y_low])
    cos, sin = phases(y, ky, NY, 1.0)
    y_high, y_low = split_table(np.concatenate([cos, sin], axis=1) / NY)
    y_back = np.concatenate([y_high, y_low], axis=1)
    cos, sin = phases(x, kx, NX, -1.0)
    x_forward = split_table(np.block([[cos, sin], [-sin, cos]]))
    cos, sin = phases(kx, x, NX, 1.0)
    x_back = split_table(np.block([[cos, sin], [-sin, cos]]) / NX)
    cos, sin = phases(kz, z, NZ, -1.0)
    z_forward = split_table(np.block([[cos, -sin], [sin, cos]]))
    cos, sin = phases(z, kz, NZ, 1.0)
    z_back = split_table(np.block([[cos, -sin], [sin, cos]]) / NZ)
    return y_forward, y_back, x_forward, x_back, z_forward, z_back


def halves(values):
    high = values.astype(BF16)
    return high, (values - high.astype(F32)).astype(BF16)


def thirds(values):
    high = values.astype(BF16)
    rest = values - high.astype(F32)
    middle = rest.astype(BF16)
    return high, middle, (rest - middle.astype(F32)).astype(BF16)


def dot(left, right):
    return jnp.dot(left, right, preferred_element_type=F32)


def dot_split(left, right):
    return dot(left[0], right[0]) + (dot(left[0], right[1]) + dot(left[1], right[0]))


def pick_rows(hot, values):
    high, middle, low = thirds(values)
    return dot(hot, high) + dot(hot, middle) + dot(hot, low)


def grid_index(shape, axis):
    return lax.broadcasted_iota(jnp.int32, shape, axis)


def to_column(row):
    n = row.shape[1]
    diagonal = grid_index((n, n), 0) == grid_index((n, n), 1)
    return jnp.sum(jnp.where(diagonal, row, 0), axis=1, keepdims=True)


def row_targets(site_ref):
    cell_y = site_ref[0:1, :]
    cell_z = site_ref[1:2, :]
    block = jnp.where(cell_y >= 0, cell_z // 2, -1)
    n = block.shape[1]
    earlier = grid_index((n, n), 0) < grid_index((n, n), 1)
    same = (to_column(block) == block) & earlier
    rank = jnp.sum(same.astype(jnp.int32), axis=0, keepdims=True)
    target = jnp.where(cell_y >= 0, rank * BLOCKS + block, -1)
    return target, (cell_z % 2) * (NY // 2) + cell_y


def pack_kernel(site_ref, dipoles_ref, out_ref):
    target, place = row_targets(site_ref)
    n = target.shape[1]
    chosen = grid_index((n, n), 0) == target
    hot = chosen.astype(BF16)
    for c in range(6):
        v, j = divmod(c, 3)
        rows = pick_rows(hot, dipoles_ref[c])
        for t in range(2):
            for p in range(2):
                out_ref[pl.ds(13 * v + 6 * t + 2 * j + p, BLOCKS, stride=26), :] = rows[
                    t * BLOCKS : (t + 1) * BLOCKS, p * LX : (p + 1) * LX
                ]
    places = jnp.sum(jnp.where(chosen, place + 1, 0), axis=1, keepdims=True) - 1
    places = places.astype(F32)
    lanes = grid_index((BLOCKS, LX), 1)
    row = jnp.where(lanes == 0, places[:BLOCKS], places[BLOCKS:])
    for v in range(2):
        out_ref[pl.ds(13 * v + 12, BLOCKS, stride=26), :] = row


def slot_places(received_ref):
    rows = received_ref[pl.ds(12, DEVICES, stride=13), :]
    return jnp.concatenate([rows[:, 0:1], rows[:, 1:2]], axis=0).astype(jnp.int32)


def y_forward_kernel(received_ref, table_ref, out_ref):
    slots = 2 * DEVICES
    column = slot_places(received_ref)
    diagonal = grid_index((slots, slots), 0) == grid_index((slots, slots), 1)
    row = jnp.sum(jnp.where(diagonal, column, 0), axis=0, keepdims=True)
    y = grid_index((NY // 2, slots), 0)
    hot = jnp.concatenate([(y == row).astype(BF16), (y + NY // 2 == row).astype(BF16)], axis=1)
    table = dot(table_ref[...], hot).astype(BF16)
    lefts = []
    for part in range(2):
        cos = table[part * 256 : part * 256 + 128]
        sin = table[part * 256 + 128 : part * 256 + 256]
        rows = []
        for zp in range(2):
            c = cos[:, zp * slots : (zp + 1) * slots]
            s = sin[:, zp * slots : (zp + 1) * slots]
            rows.append(jnp.concatenate([c, -s], axis=1))
            rows.append(jnp.concatenate([s, c], axis=1))
        lefts.append(jnp.concatenate(rows, axis=0))
    rights = []
    for j in range(3):
        pieces = []
        for p in range(2):
            for t in range(2):
                pieces.append(received_ref[pl.ds(6 * t + 2 * j + p, DEVICES, stride=13), :])
        rights.append(jnp.concatenate(pieces, axis=0))
    right = halves(jnp.concatenate(rights, axis=1))
    result = dot_split(lefts, right)
    for zp in range(2):
        for p in range(2):
            for j in range(3):
                out_ref[pl.ds(6 * zp + 2 * j + p, NY, stride=12), :] = result[
                    zp * 256 + p * 128 : zp * 256 + p * 128 + 128, j * 128 : (j + 1) * 128
                ]


SYMMETRIC = ((0, 1, 2), (1, 3, 4), (2, 4, 5))


def middle_kernel(
    received_ref,
    green_ref,
    xf_high,
    xf_low,
    xb_high,
    xb_low,
    zf_high,
    zf_low,
    zb_high,
    zb_low,
    out_ref,
):
    for g in range(4):
        ky = g % 2
        base = 12 * g
        rows = []
        for j in range(3):
            lanes = []
            for p in range(2):
                lanes.append(
                    jnp.concatenate(
                        [
                            received_ref[pl.ds(base + 6 * zp + 2 * j + p, BLOCKS, stride=48), :]
                            for zp in range(2)
                        ],
                        axis=0,
                    )
                )
            rows.append(jnp.concatenate(lanes, axis=1))
        lines = halves(jnp.concatenate(rows, axis=0))
        lines = dot_split(lines, (xf_high[...], xf_low[...]))
        planes = jnp.concatenate(
            [
                jnp.concatenate([lines[64 * j : 64 * j + 64, :NX], lines[64 * j : 64 * j + 64, NX:]], axis=0)
                for j in range(3)
            ],
            axis=1,
        )
        planes = dot_split((zf_high[...], zf_low[...]), halves(planes))
        images_re = []
        images_im = []
        for a in range(3):
            total_re = None
            for b in range(3):
                m = SYMMETRIC[a][b]
                kernel_re = green_ref[ky, m, :, :NX]
                kernel_im = green_ref[ky, m, :, NX:]
                source_re = planes[:NZ, b * NX : (b + 1) * NX]
                source_im = planes[NZ:, b * NX : (b + 1) * NX]
                term_re = kernel_re * source_re - kernel_im * source_im
                term_im = kernel_re * source_im + kernel_im * source_re
                total_re = term_re if b == 0 else total_re + term_re
                total_im = term_im if b == 0 else total_im + term_im
            images_re.append(total_re)
            images_im.append(total_im)
        images = jnp.concatenate(
            [jnp.concatenate(images_re, axis=1), jnp.concatenate(images_im, axis=1)], axis=0
        )
        planes = dot_split((zb_high[...], zb_low[...]), halves(images))
        lines = jnp.concatenate(
            [
                jnp.concatenate(
                    [planes[:64, j * NX : (j + 1) * NX], planes[64:, j * NX : (j + 1) * NX]], axis=1
                )
                for j in range(3)
            ],
            axis=0,
        )
        lines = dot_split(halves(lines), (xb_high[...], xb_low[...]))
        for j in range(3):
            for p in range(2):
                for zp in range(2):
                    first = 64 * j + BLOCKS * zp
                    out_ref[pl.ds(base + 6 * zp + 2 * j + p, BLOCKS, stride=48), :] = lines[
                        first : first + BLOCKS, p * LX : (p + 1) * LX
                    ]


def y_back_kernel(received_ref, first_ref, table_ref, out_ref):
    slots = 2 * DEVICES
    column = slot_places(first_ref)
    y = grid_index((slots, NY // 2), 1)
    hot = jnp.concatenate([(y == column).astype(BF16), (y + NY // 2 == column).astype(BF16)], axis=0)
    table = dot(hot, table_ref[...]).astype(BF16)
    lefts = []
    for part in range(2):
        cos = table[:, part * 256 : part * 256 + 128]
        sin = table[:, part * 256 + 128 : part * 256 + 256]
        c0, c1, s0, s1 = cos[:slots], cos[slots:], sin[:slots], sin[slots:]
        lefts.append(
            jnp.concatenate(
                [
                    jnp.concatenate([c0, c1, -s0, -s1], axis=1),
                    jnp.concatenate([s0, s1, c0, c1], axis=1),
                ],
                axis=0,
            )
        )
    rights = []
    for j in range(3):
        pieces = []
        for p in range(2):
            for zp in range(2):
                pieces.append(received_ref[pl.ds(6 * zp + 2 * j + p, NY, stride=12), :])
        rights.append(jnp.concatenate(pieces, axis=0))
    right = halves(jnp.concatenate(rights, axis=1))
    result = dot_split(lefts, right)
    for p in range(2):
        for t in range(2):
            for j in range(3):
                first = p * slots + t * DEVICES
                out_ref[pl.ds(6 * t + 2 * j + p, DEVICES, stride=12), :] = result[
                    first : first + DEVICES, j * 128 : (j + 1) * 128
                ]


def finish_kernel(received_ref, site_ref, dipoles_ref, alpha_ref, out_ref):
    target, _ = row_targets(site_ref)
    n = target.shape[1]
    target = to_column(target)
    hot = (grid_index((n, n), 1) == target).astype(BF16)
    live = target >= 0
    alpha_re = alpha_ref[:, :LX]
    alpha_im = alpha_ref[:, LX:]
    for c in range(6):
        v, j = divmod(c, 3)
        lanes = []
        for p in range(2):
            lanes.append(
                jnp.concatenate(
                    [
                        received_ref[pl.ds(12 * v + 6 * t + 2 * j + p, BLOCKS, stride=24), :]
                        for t in range(2)
                    ],
                    axis=0,
                )
            )
        rows = pick_rows(hot, jnp.concatenate(lanes, axis=1))
        dip_re = dipoles_ref[c, :, :LX]
        dip_im = dipoles_ref[c, :, LX:]
        out_ref[c, :, :LX] = jnp.where(live, alpha_re * dip_re - alpha_im * dip_im - rows[:, :LX], 0.0)
        out_ref[c, :, LX:] = jnp.where(live, alpha_re * dip_im + alpha_im * dip_re - rows[:, LX:], 0.0)


def call(kernel, shape, *operands, flops=0):
    whole = pl.BlockSpec(memory_space=pltpu.VMEM)
    return pl.pallas_call(
        kernel,
        out_shape=jax.ShapeDtypeStruct(shape, F32),
        in_specs=[whole] * len(operands),
        out_specs=whole,
        compiler_params=pltpu.CompilerParams(vmem_limit_bytes=48 * 1024 * 1024),
        cost_estimate=pl.CostEstimate(flops=flops, bytes_accessed=0, transcendentals=0),
        interpret=INTERPRET,
    )(*operands)


def exchange(rows):
    packed = rows.reshape(DEVICES, 1, rows.shape[0] // DEVICES * rows.shape[1])
    moved = lax.all_to_all(packed, "slab", split_axis=0, concat_axis=0, tiled=True)
    return moved.reshape(rows.shape)


def body(dipoles, inv_alpha, row_site, green):
    y_forward, y_back, x_forward, x_back, z_forward, z_back = tables()
    packed = call(pack_kernel, (13 * DEVICES, LX), row_site, dipoles)
    first = exchange(packed)
    planes = call(y_forward_kernel, (24 * DEVICES, LX), first, y_forward)
    pencils = exchange(planes)
    green_rows = jnp.transpose(green, (2, 0, 1, 3))
    images = call(
        middle_kernel,
        (24 * DEVICES, LX),
        pencils,
        green_rows,
        *x_forward,
        *x_back,
        *z_forward,
        *z_back,
    )
    planes = exchange(images)
    rows = call(y_back_kernel, (12 * DEVICES, LX), planes, first, y_back)
    returned = exchange(rows)
    return call(finish_kernel, dipoles.shape, returned, row_site, dipoles, inv_alpha)


def solution(mesh):
    return jax.shard_map(
        body,
        mesh=mesh,
        in_specs=(
            P("rep", "slab", None),
            P("slab", None),
            P(None, "slab"),
            P(None, None, "slab", None),
        ),
        out_specs=P("rep", "slab", None),
        check_vma=False,
    )
```

time: 238 us -> 128 us (0.54); the launches traced: 235 us -> 127 us
  waiting for transfers between devices: 131 us -> 20.4 us
  blocking collectives: 0 us -> 78.2 us
  matrix products: 36.1 us -> 0 us
  starting transfers between devices: 38.1 us -> 5.77 us
  Pallas kernels: 0 us -> 12.4 us
  other arithmetic: 9.07 us -> 0 us
  local copies, waits for them, and re-layouts: 19.3 us -> 10.5 us
    all_to_all x5 -> x1, waiting for transfers between devices: 131 us -> 20.4 us  [exchange(): lax.all_to_all(packed, 'slab', split_axis=0, concat_axis=0, tiled=True)]
    all_to_all x0 -> x3, blocking collectives: none -> 78.2 us  [exchange(): lax.all_to_all(packed, 'slab', split_axis=0, concat_axis=0, tiled=True)]
    dot_general x14 -> x0, matrix products: 36.1 us -> none  [the longest x4 14 us: middle_transform(): mixed_cos = jnp.einsum(pattern, cosine, values, precision=HIGH)]
    all_to_all x5 -> x1, starting transfers between devices: 38.1 us -> 5.77 us  [exchange(): lax.all_to_all(packed, 'slab', split_axis=0, concat_axis=0, tiled=True)]
    pallas_call x0 -> x5, Pallas kernels: none -> 12.4 us  [call(): pl.pallas_call(kernel, out_shape=jax.ShapeDtypeStruct(shape, F32), in_spe...]
    concatenate x2 -> x0, local copies, waits for them, and re-layouts: 5.44 us -> none  [middle_transform(): return jnp.concatenate([real_part, imag_part], axis=-1)]
    unnamed x21 -> x35, local copies, waits for them, and re-layouts: 6.3 us -> 10.5 us
  transfers between devices with their start and end apart: 5 -> 1, of which waited for: 5 -> 1; matrix products, arithmetic and copies ran while one was open for 5% -> 2% of each run, Pallas kernels for 0% -> 0%
where the time goes in v1:
time: 128 us; the launch traced here: 127 us
  blocking collectives  78.2 us (61%)
  waiting for transfers between devices  20.4 us (16%)
  Pallas kernels  12.4 us (10%)
  local copies, waits for them, and re-layouts  10.5 us (8%)
  starting transfers between devices  5.77 us (5%)
    all_to_all x3, blocking collectives, exchange(): lax.all_to_all(packed, 'slab', split_axis=0, concat_axis=0, tiled=True)  78.2 us
    all_to_all x1, waiting for transfers between devices, exchange(): lax.all_to_all(packed, 'slab', split_axis=0, concat_axis=0, tiled=True)  20.4 us
    pallas_call x5, Pallas kernels, call(): pl.pallas_call(kernel, out_shape=jax.ShapeDtypeStruct(shape, F32), in_spe...  12.4 us
    unnamed x35, local copies, waits for them, and re-layouts  10.5 us
    all_to_all x1, starting transfers between devices, exchange(): lax.all_to_all(packed, 'slab', split_axis=0, concat_axis=0, tiled=True)  5.77 us
  transfers between devices with their start and end apart: 1, of which 1 were waited for; matrix products, arithmetic and copies ran while one was open for 2% of the time, Pallas kernels for 0%

profile of v1, /device:TPU:1, one launch (start us, length us, event | category | flops | bytes accessed | tf_op | source)
XLA Modules:
  0.0 127.3 jit_solution(16129844079721813825)
XLA Ops:
  0.0 1.0 copy-done.2
  1.0 0.7 copy-done.15
  1.7 0.4 shard_map.136
  2.1 28.5 %all_to_all.20 = f32[64,1,1664]{2,1,0:T(1,128)S(1)} all-to-all(f32[64,1,1664]{2,1,0:T(1,128)S(1)} %bitcast.16), channel_id=1, replica_groups=mesh['slab'=64,'rep'=4] {'slab'}, dimensions={0} | all-to-all | bytes 851968 | tf_op jit(solution)/shard_map/all_to_all | solution.py:330
  30.6 0.9 copy-done.8
  31.5 1.8 %shard_map.137 = f32[1536,128]{1,0:T(8,128)} custom-call(f32[832,128]{1,0:T(8,128)S(1)} %bitcast.12, bf16[512,64]{1,0:T(8,128)(2,1)S(1)} %copy-done.8), custom_call_target="tpu_custom_call" | custom-call | tf_op jit(solution)/shard_map/pallas_call | solution.py:317
  33.2 0.8 copy-done
  34.0 5.8 %all-to-all-start.1 = ((f32[64,1,3072]{2,1,0:T(1,128)}), f32[64,1,3072]{2,1,0:T(1,128)}, u32[]{:S(2)}, u32[]{:S(2)}) async-start(f32[64,1,3072]{2,1,0:T(1,128)} %bitcast.2), calls=%async_computation.1 | async-start | bytes 1572864 | tf_op jit(solution)/shard_map/all_to_all | solution.py:330
  39.8 0.0 copy-start.4
  39.8 0.0 copy-start.9
  39.8 0.0 copy-start.10
  39.8 2.5 %copy.22 = f32[6,128,2,512]{3,1,0,2:T(8,128)S(1)} copy(f32[6,128,2,512]{3,2,1,0:T(2,128)} %param.17) | data formatting | bytes 6291456 | tf_op args[3]
  42.4 20.4 %all-to-all-done.1 = f32[64,1,3072]{2,1,0:T(1,128)} async-done(((f32[64,1,3072]{2,1,0:T(1,128)}), f32[64,1,3072]{2,1,0:T(1,128)}, u32[]{:S(2)}, u32[]{:S(2)}) %all-to-all-start.1) | async-done | bytes 786464 | tf_op jit(solution)/shard_map/all_to_all | solution.py:330
  62.7 0.0 copy-done.4
  62.7 0.0 copy-done.9
  62.7 0.0 copy-done.10
  62.7 0.0 copy-start.5
  62.7 0.9 copy-done.5
  63.7 0.9 copy-done.6
  64.6 0.9 copy-done.7
  65.6 0.8 copy-done.11
  66.4 0.8 copy-done.12
  67.3 8.1 %shard_map.138 = f32[1536,128]{1,0:T(8,128)S(1)} custom-call(f32[1536,128]{1,0:T(8,128)} %bitcast.3.received_ref, f32[2,6,128,512]{3,2,1,0:T(8,128)S(1)} %bitcast.11, bf16[256,512]{1,0:T(8,128)(2,1)S(1)} %copy-done.7, bf16[256,512]{1,0:T(8,128)(2,1)S(1)} %copy-done.6, bf16[512,256]{1,0:T(8,128)(2,1)S(1)} %copy-done.5, bf16[512,256]{1,0:T(8,128)(2,1)S(1)} %copy-done.4, ...), custom_call_target="tpu_custom_call" | custom-call | tf_op jit(solution)/shard_map/pallas_call | solution.py:317
  75.4 0.0 copy-start.3
  75.4 0.0 copy-start.13
  75.4 0.0 copy-start.16
  75.5 28.8 %all_to_all.21 = f32[64,1,3072]{2,1,0:T(1,128)S(1)} all-to-all(f32[64,1,3072]{2,1,0:T(1,128)S(1)} %bitcast.15), channel_id=1, replica_groups=mesh['slab'=64,'rep'=4] {'slab'}, dimensions={0} | all-to-all | bytes 1572864 | tf_op jit(solution)/shard_map/all_to_all | solution.py:330
  104.3 0.0 copy-done.1
  104.3 0.8 shard_map.139
  105.1 20.9 %all_to_all.22 = f32[64,1,1536]{2,1,0:T(1,128)S(1)} all-to-all(f32[64,1,1536]{2,1,0:T(1,128)S(1)} %bitcast.17), channel_id=1, replica_groups=mesh['slab'=64,'rep'=4] {'slab'}, dimensions={0} | all-to-all | bytes 786432 | tf_op jit(solution)/shard_map/all_to_all | solution.py:330
  126.0 0.0 copy-done.13
  126.0 1.3 shard_map.140
  (13 shorter events, 0.0 us)
Async XLA Ops:
  0.0 1.0 copy-start.2
  1.0 0.7 copy-start.15
  30.6 0.9 copy-start.8
  33.2 0.8 copy-start
  34.0 28.7 %all-to-all-start.1 = ((f32[64,1,3072]{2,1,0:T(1,128)}), f32[64,1,3072]{2,1,0:T(1,128)}, u32[]{:S(2)}, u32[]{:S(2)}) async-start(f32[64,1,3072]{2,1,0:T(1,128)} %bitcast.2), calls=%async_computation.1 | async-start | bytes 1572864 | tf_op jit(solution)/shard_map/all_to_all | solution.py:330
  39.8 22.9 %copy-start.4 = (bf16[512,256]{1,0:T(8,128)(2,1)S(1)}, bf16[512,256]{1,0:T(8,128)(2,1)}, u32[]{:S(2)}) copy-start(bf16[512,256]{1,0:T(8,128)(2,1)} %constant.24.clone.xb_low) | copy-start | bytes 786436
  39.8 22.9 %copy-start.9 = (bf16[128,256]{1,0:T(8,128)(2,1)S(1)}, bf16[128,256]{1,0:T(8,128)(2,1)}, u32[]{:S(2)}) copy-start(bf16[128,256]{1,0:T(8,128)(2,1)} %constant.28.clone.zb_low) | copy-start | bytes 196612
  39.8 22.9 %copy-start.10 = (bf16[128,256]{1,0:T(8,128)(2,1)S(1)}, bf16[128,256]{1,0:T(8,128)(2,1)}, u32[]{:S(2)}) copy-start(bf16[128,256]{1,0:T(8,128)(2,1)} %constant.27.clone.zb_high) | copy-start | bytes 196612
  62.7 1.0 copy-start.5
  63.7 0.9 copy-start.6
  64.6 0.9 copy-start.7
  65.6 0.8 copy-start.11
  66.4 0.8 copy-start.12
  67.3 37.0 %copy-start.1 = (f32[64,1,1664]{2,1,0:T(1,128)S(1)}, f32[64,1,1664]{2,1,0:T(1,128)}, u32[]{:S(2)}) copy-start(f32[64,1,1664]{2,1,0:T(1,128)} %copy-done) | copy-start | bytes 1277956
  67.3 37.0 %copy-start.14 = (bf16[64,512]{1,0:T(8,128)(2,1)S(1)}, bf16[64,512]{1,0:T(8,128)(2,1)}, u32[]{:S(2)}) copy-start(bf16[64,512]{1,0:T(8,128)(2,1)} %constant.29.clone.table_ref) | copy-start | bytes 196612
  75.4 50.6 %copy-start.3 = (f32[6,64,256]{2,1,0:T(8,128)S(1)}, f32[6,64,256]{2,1,0:T(8,128)}, u32[]{:S(2)}) copy-start(f32[6,64,256]{2,1,0:T(8,128)} %dipoles_ref.3) | copy-start | bytes 1179652
  75.4 50.6 %copy-start.13 = (f32[64,256]{1,0:T(8,128)S(1)}, f32[64,256]{1,0:T(8,128)}, u32[]{:S(2)}) copy-start(f32[64,256]{1,0:T(8,128)} %alpha_ref.1) | copy-start | bytes 196612
  75.4 50.6 %copy-start.16 = (s32[2,64]{1,0:T(2,128)S(1)}, s32[2,64]{1,0:T(2,128)}, u32[]{:S(2)}) copy-start(s32[2,64]{1,0:T(2,128)} %site_ref.3) | copy-start | bytes 1540

commit v2 on v1

--- a/solution.py
+++ b/solution.py
@@ -52,7 +52,19 @@
     z_forward = split_table(np.block([[cos, -sin], [sin, cos]]))
     cos, sin = phases(z, kz, NZ, 1.0)
     z_back = split_table(np.block([[cos, -sin], [sin, cos]]) / NZ)
-    return y_forward, y_back, x_forward, x_back, z_forward, z_back
+    y_rows = np.zeros((384, 256), BF16)
+    y_rows[:256, :64] = y_forward[:256]
+    y_rows[:256, 64:128] = y_forward[256:]
+    y_rows[256:320] = y_back[:, :256]
+    y_rows[320:384] = y_back[:, 256:]
+    pieces = []
+    for part in x_forward:
+        pieces += [part[:, :NX], part[:, NX:]]
+    for part in x_back:
+        pieces += [part[:NX], part[NX:]]
+    pieces.append(np.concatenate(z_forward, axis=1))
+    pieces.append(np.concatenate(z_back, axis=0))
+    return y_rows, np.stack(pieces)
 
 
 def halves(values):
@@ -123,23 +135,26 @@
         out_ref[pl.ds(13 * v + 12, BLOCKS, stride=26), :] = row
 
 
-def slot_places(received_ref):
-    rows = received_ref[pl.ds(12, DEVICES, stride=13), :]
+def slot_places(rows):
     return jnp.concatenate([rows[:, 0:1], rows[:, 1:2]], axis=0).astype(jnp.int32)
 
 
-def y_forward_kernel(received_ref, table_ref, out_ref):
+def y_forward_kernel(received_ref, table_ref, out_ref, places_ref):
     slots = 2 * DEVICES
-    column = slot_places(received_ref)
+    places = received_ref[pl.ds(12, DEVICES, stride=13), :]
+    places_ref[...] = places
+    column = slot_places(places)
     diagonal = grid_index((slots, slots), 0) == grid_index((slots, slots), 1)
     row = jnp.sum(jnp.where(diagonal, column, 0), axis=0, keepdims=True)
     y = grid_index((NY // 2, slots), 0)
     hot = jnp.concatenate([(y == row).astype(BF16), (y + NY // 2 == row).astype(BF16)], axis=1)
-    table = dot(table_ref[...], hot).astype(BF16)
+    none = jnp.zeros_like(hot)
     lefts = []
     for part in range(2):
-        cos = table[part * 256 : part * 256 + 128]
-        sin = table[part * 256 + 128 : part * 256 + 256]
+        chooser = jnp.concatenate([none, hot] if part else [hot, none], axis=0)
+        table = dot(table_ref[:256, :128], chooser).astype(BF16)
+        cos = table[:128]
+        sin = table[128:]
         rows = []
         for zp in range(2):
             c = cos[:, zp * slots : (zp + 1) * slots]
@@ -167,19 +182,7 @@
 SYMMETRIC = ((0, 1, 2), (1, 3, 4), (2, 4, 5))
 
 
-def middle_kernel(
-    received_ref,
-    green_ref,
-    xf_high,
-    xf_low,
-    xb_high,
-    xb_low,
-    zf_high,
-    zf_low,
-    zb_high,
-    zb_low,
-    out_ref,
-):
+def middle_kernel(received_ref, green_ref, table_ref, out_ref):
     for g in range(4):
         ky = g % 2
         base = 12 * g
@@ -198,23 +201,26 @@
                 )
             rows.append(jnp.concatenate(lanes, axis=1))
         lines = halves(jnp.concatenate(rows, axis=0))
-        lines = dot_split(lines, (xf_high[...], xf_low[...]))
+        lines = [dot_split(lines, (table_ref[p], table_ref[2 + p])) for p in range(2)]
         planes = jnp.concatenate(
-            [
-                jnp.concatenate([lines[64 * j : 64 * j + 64, :NX], lines[64 * j : 64 * j + 64, NX:]], axis=0)
-                for j in range(3)
-            ],
+            [jnp.concatenate([lines[p][64 * j : 64 * j + 64] for p in range(2)], axis=0) for j in range(3)],
             axis=1,
         )
-        planes = dot_split((zf_high[...], zf_low[...]), halves(planes))
+        high, low = halves(planes)
+        planes = dot(table_ref[8], jnp.concatenate([high, high], axis=0)) + dot(table_ref[8, :, :128], low)
         images_re = []
         images_im = []
         for a in range(3):
             total_re = None
             for b in range(3):
                 m = SYMMETRIC[a][b]
-                kernel_re = green_ref[ky, m, :, :NX]
-                kernel_im = green_ref[ky, m, :, NX:]
+                kernel_re, kernel_im = [
+                    jnp.concatenate(
+                        [green_ref[pl.ds(8 * NZ * m + 4 * p + 2 * h + ky, NZ, stride=8), :] for h in range(2)],
+                        axis=1,
+                    )
+                    for p in range(2)
+                ]
                 source_re = planes[:NZ, b * NX : (b + 1) * NX]
                 source_im = planes[NZ:, b * NX : (b + 1) * NX]
                 term_re = kernel_re * source_re - kernel_im * source_im
@@ -226,17 +232,14 @@
         images = jnp.concatenate(
             [jnp.concatenate(images_re, axis=1), jnp.concatenate(images_im, axis=1)], axis=0
         )
-        planes = dot_split((zb_high[...], zb_low[...]), halves(images))
-        lines = jnp.concatenate(
-            [
-                jnp.concatenate(
-                    [planes[:64, j * NX : (j + 1) * NX], planes[64:, j * NX : (j + 1) * NX]], axis=1
-                )
-                for j in range(3)
-            ],
-            axis=0,
-        )
-        lines = dot_split(halves(lines), (xb_high[...], xb_low[...]))
+        planes = dot_split((table_ref[9, :128], table_ref[9, 128:]), halves(images))
+        lines = None
+        for p in range(2):
+            part = jnp.concatenate(
+                [planes[64 * p : 64 * p + 64, j * NX : (j + 1) * NX] for j in range(3)], axis=0
+            )
+            part = dot_split(halves(part), (table_ref[4 + p], table_ref[6 + p]))
+            lines = part if p == 0 else lines + part
         for j in range(3):
             for p in range(2):
                 for zp in range(2):
@@ -246,16 +249,16 @@
                     ]
 
 
-def y_back_kernel(received_ref, first_ref, table_ref, out_ref):
+def y_back_kernel(received_ref, places_ref, table_ref, out_ref):
     slots = 2 * DEVICES
-    column = slot_places(first_ref)
+    column = slot_places(places_ref[...])
     y = grid_index((slots, NY // 2), 1)
     hot = jnp.concatenate([(y == column).astype(BF16), (y + NY // 2 == column).astype(BF16)], axis=0)
-    table = dot(hot, table_ref[...]).astype(BF16)
     lefts = []
     for part in range(2):
-        cos = table[:, part * 256 : part * 256 + 128]
-        sin = table[:, part * 256 + 128 : part * 256 + 256]
+        table = dot(hot, table_ref[256 + 64 * part : 320 + 64 * part, :]).astype(BF16)
+        cos = table[:, :128]
+        sin = table[:, 128:]
         c0, c1, s0, s1 = cos[:slots], cos[slots:], sin[:slots], sin[slots:]
         lefts.append(
             jnp.concatenate(
@@ -312,17 +315,17 @@
         out_ref[c, :, LX:] = jnp.where(live, alpha_re * dip_im + alpha_im * dip_re - rows[:, LX:], 0.0)
 
 
-def call(kernel, shape, *operands, flops=0):
+def call(kernel, shape, *operands, megabytes, flops=0, **more):
     whole = pl.BlockSpec(memory_space=pltpu.VMEM)
-    return pl.pallas_call(
-        kernel,
-        out_shape=jax.ShapeDtypeStruct(shape, F32),
+    options = dict(
+        out_shape=shape and jax.ShapeDtypeStruct(shape, F32),
         in_specs=[whole] * len(operands),
         out_specs=whole,
-        compiler_params=pltpu.CompilerParams(vmem_limit_bytes=48 * 1024 * 1024),
-        cost_estimate=pl.CostEstimate(flops=flops, bytes_accessed=0, transcendentals=0),
+        compiler_params=pltpu.CompilerParams(vmem_limit_bytes=megabytes * 1024 * 1024),
+        cost_estimate=pl.CostEstimate(flops=2000000000, bytes_accessed=20000000, transcendentals=0),
         interpret=INTERPRET,
-    )(*operands)
+    )
+    return pl.pallas_call(kernel, **{**options, **more})(*operands)
 
 
 def exchange(rows):
@@ -332,26 +335,28 @@
 
 
 def body(dipoles, inv_alpha, row_site, green):
-    y_forward, y_back, x_forward, x_back, z_forward, z_back = tables()
-    packed = call(pack_kernel, (13 * DEVICES, LX), row_site, dipoles)
+    y_table, table = tables()
+    packed = call(pack_kernel, (13 * DEVICES, LX), row_site, dipoles, megabytes=4)
     first = exchange(packed)
-    planes = call(y_forward_kernel, (24 * DEVICES, LX), first, y_forward)
+    planes, places = call(
+        y_forward_kernel,
+        None,
+        first,
+        y_table,
+        megabytes=8,
+        out_shape=(
+            jax.ShapeDtypeStruct((24 * DEVICES, LX), F32),
+            jax.ShapeDtypeStruct((DEVICES, LX), F32),
+        ),
+        out_specs=(pl.BlockSpec(memory_space=pltpu.VMEM), pl.BlockSpec(memory_space=pltpu.VMEM)),
+    )
     pencils = exchange(planes)
-    green_rows = jnp.transpose(green, (2, 0, 1, 3))
-    images = call(
-        middle_kernel,
-        (24 * DEVICES, LX),
-        pencils,
-        green_rows,
-        *x_forward,
-        *x_back,
-        *z_forward,
-        *z_back,
-    )
+    green_rows = green.reshape(6, NZ, 2, 4, LX).transpose(0, 1, 3, 2, 4).reshape(48 * NZ, LX)
+    images = call(middle_kernel, (24 * DEVICES, LX), pencils, green_rows, table, megabytes=16)
     planes = exchange(images)
-    rows = call(y_back_kernel, (12 * DEVICES, LX), planes, first, y_back)
+    rows = call(y_back_kernel, (12 * DEVICES, LX), planes, places, y_table, megabytes=8)
     returned = exchange(rows)
-    return call(finish_kernel, dipoles.shape, returned, row_site, dipoles, inv_alpha)
+    return call(finish_kernel, dipoles.shape, returned, row_site, dipoles, inv_alpha, megabytes=4)
 
 
 def solution(mesh):

time: 128 us -> 119 us (0.930)
  blocking collectives: 78.2 us -> 107 us
  waiting for transfers between devices: 20.4 us -> 0 us
  local copies, waits for them, and re-layouts: 10.5 us -> 1.7 us
  starting transfers between devices: 5.77 us -> 0 us
  Pallas kernels: 12.4 us -> 10.2 us
    all_to_all x3 -> x4, blocking collectives: 78.2 us -> 107 us  [exchange(): lax.all_to_all(packed, 'slab', split_axis=0, concat_axis=0, tiled=True)]
    all_to_all x1 -> x0, waiting for transfers between devices: 20.4 us -> none  [exchange(): lax.all_to_all(packed, 'slab', split_axis=0, concat_axis=0, tiled=True)]
    unnamed x35 -> x16, local copies, waits for them, and re-layouts: 10.5 us -> 1.7 us
    all_to_all x1 -> x0, starting transfers between devices: 5.77 us -> none  [exchange(): lax.all_to_all(packed, 'slab', split_axis=0, concat_axis=0, tiled=True)]
    pallas_call x5, Pallas kernels: 12.4 us -> 10.2 us  [call(): return pl.pallas_call(kernel, **{**options, **more})(*operands)]
  transfers between devices with their start and end apart: 1 -> 0, of which waited for: 1 -> 0; matrix products, arithmetic and copies ran while one was open for 2% -> 0% of each run, Pallas kernels for 0% -> 0%
where the time goes in v2:
time: 119 us; the launch traced here: 118 us
  blocking collectives  107 us (90%)
  Pallas kernels  10.2 us (9%)
  local copies, waits for them, and re-layouts  1.7 us (1%)
    all_to_all x4, blocking collectives, exchange(): lax.all_to_all(packed, 'slab', split_axis=0, concat_axis=0, tiled=True)  107 us
    pallas_call x5, Pallas kernels, call(): return pl.pallas_call(kernel, **{**options, **more})(*operands)  10.2 us

profile of v2, /device:TPU:1, one launch (start us, length us, event | category | flops | bytes accessed | tf_op | source)
XLA Modules:
  0.0 118.5 jit_solution(16040102394248038286)
XLA Ops:
  0.0 0.0 copy-start.1
  0.0 1.0 copy-done.1
  1.0 0.0 copy-start.4
  1.0 0.7 copy-done.4
  1.7 0.0 copy-start.7
  1.7 0.4 shard_map.64
  2.1 28.5 %all_to_all.20 = f32[64,1,1664]{2,1,0:T(1,128)S(1)} all-to-all(f32[64,1,1664]{2,1,0:T(1,128)S(1)} %bitcast.18), channel_id=1, replica_groups=mesh['slab'=64,'rep'=4] {'slab'}, dimensions={0} | all-to-all | bytes 851968 | tf_op jit(solution)/shard_map/all_to_all | solution.py:333
  30.6 0.0 copy-done.7
  30.6 0.0 copy-start
  30.6 0.0 copy-start.6
  30.6 0.9 shard_map.65
  31.4 28.5 %all_to_all.21 = f32[64,1,3072]{2,1,0:T(1,128)S(1)} all-to-all(f32[64,1,3072]{2,1,0:T(1,128)S(1)} %bitcast.14), channel_id=1, replica_groups=mesh['slab'=64,'rep'=4] {'slab'}, dimensions={0} | all-to-all | bytes 1572864 | tf_op jit(solution)/shard_map/all_to_all | solution.py:333
  60.0 0.0 copy-done
  60.0 0.0 copy-done.6
  60.0 6.8 %shard_map.66 = f32[1536,128]{1,0:T(8,128)S(1)} custom-call(f32[1536,128]{1,0:T(8,128)S(1)} %bitcast.15, f32[6144,128]{1,0:T(8,128)S(1)} %bitcast.21, bf16[10,256,256]{2,1,0:T(8,128)(2,1)S(1)} %copy-done.6), custom_call_target="tpu_custom_call" | custom-call | flops 2000000000 | bytes 20000000 | tf_op jit(solution)/shard_map/pallas_call | solution.py:328
  66.8 28.7 %all_to_all.22 = f32[64,1,3072]{2,1,0:T(1,128)S(1)} all-to-all(f32[64,1,3072]{2,1,0:T(1,128)S(1)} %bitcast.16), channel_id=1, replica_groups=mesh['slab'=64,'rep'=4] {'slab'}, dimensions={0} | all-to-all | bytes 1572864 | tf_op jit(solution)/shard_map/all_to_all | solution.py:333
  95.5 0.0 copy-start.2
  95.5 0.0 copy-start.3
  95.5 0.0 copy-start.5
  95.5 0.8 shard_map.67
  96.3 20.9 %all_to_all.23 = f32[64,1,1536]{2,1,0:T(1,128)S(1)} all-to-all(f32[64,1,1536]{2,1,0:T(1,128)S(1)} %bitcast.19), channel_id=1, replica_groups=mesh['slab'=64,'rep'=4] {'slab'}, dimensions={0} | all-to-all | bytes 786432 | tf_op jit(solution)/shard_map/all_to_all | solution.py:333
  117.2 0.0 copy-done.2
  117.2 0.0 copy-done.3
  117.2 0.0 copy-done.5
  117.2 1.3 %shard_map.68 = f32[6,64,256]{2,1,0:T(8,128)} custom-call(f32[768,128]{1,0:T(8,128)S(1)} %bitcast.20, s32[2,64]{1,0:T(2,128)S(1)} %copy-done.5, f32[6,64,256]{2,1,0:T(8,128)S(1)} %copy-done.2, f32[64,256]{1,0:T(8,128)S(1)} %copy-done.3), custom_call_target="tpu_custom_call" | custom-call | flops 2000000000 | bytes 20000000 | tf_op jit(solution)/shard_map/pallas_call | solution.py:328
Async XLA Ops:
  0.0 1.0 copy-start.1
  1.0 0.7 copy-start.4
  1.7 28.9 %copy-start.7 = (bf16[384,256]{1,0:T(8,128)(2,1)S(1)}, bf16[384,256]{1,0:T(8,128)(2,1)}, u32[]{:S(2)}) copy-start(bf16[384,256]{1,0:T(8,128)(2,1)} %constant.4.clone.table_ref) | copy-start | bytes 589828
  30.6 29.4 %copy-start = (f32[6,128,2,512]{3,2,1,0:T(2,128)S(1)}, f32[6,128,2,512]{3,2,1,0:T(2,128)}, u32[]{:S(2)}) copy-start(f32[6,128,2,512]{3,2,1,0:T(2,128)} %param.9) | copy-start | bytes 9437188
  30.6 29.4 %copy-start.6 = (bf16[10,256,256]{2,1,0:T(8,128)(2,1)S(1)}, bf16[10,256,256]{2,1,0:T(8,128)(2,1)}, u32[]{:S(2)}) copy-start(bf16[10,256,256]{2,1,0:T(8,128)(2,1)} %constant.5.clone.table_ref) | copy-start | bytes 3932164
  95.5 21.7 %copy-start.2 = (f32[6,64,256]{2,1,0:T(8,128)S(1)}, f32[6,64,256]{2,1,0:T(8,128)}, u32[]{:S(2)}) copy-start(f32[6,64,256]{2,1,0:T(8,128)} %dipoles_ref.3) | copy-start | bytes 1179652
  95.5 21.7 %copy-start.3 = (f32[64,256]{1,0:T(8,128)S(1)}, f32[64,256]{1,0:T(8,128)}, u32[]{:S(2)}) copy-start(f32[64,256]{1,0:T(8,128)} %alpha_ref.1) | copy-start | bytes 196612
  95.5 21.7 %copy-start.5 = (s32[2,64]{1,0:T(2,128)S(1)}, s32[2,64]{1,0:T(2,128)}, u32[]{:S(2)}) copy-start(s32[2,64]{1,0:T(2,128)} %site_ref.3) | copy-start | bytes 1540

commit v3 on v2

--- a/solution.py
+++ b/solution.py
@@ -12,8 +12,8 @@
 NY = 128
 NZ = 128
 LX = 128
-DEVICES = 64
-BLOCKS = 32
+CHIPS = 32
+SLOTS = 128
 INTERPRET = False
 
 F32 = jnp.float32
@@ -31,19 +31,28 @@
     return np.cos(angles), sign * np.sin(angles)
 
 
-def tables():
+def y_tables(core):
     y = np.arange(NY // 2)
-    ky = np.arange(NY)
-    z = np.concatenate([np.arange(0, NZ // 2, 2), np.arange(1, NZ // 2, 2)])
-    kz = np.arange(NZ)
-    x = np.arange(LX)
-    kx = np.arange(NX)
+    ky = np.arange(NY) ^ (2 * core)
     cos, sin = phases(ky, y, NY, -1.0)
     y_high, y_low = split_table(np.concatenate([cos, sin]))
     y_forward = np.concatenate([y_high, y_low])
     cos, sin = phases(y, ky, NY, 1.0)
     y_high, y_low = split_table(np.concatenate([cos, sin], axis=1) / NY)
     y_back = np.concatenate([y_high, y_low], axis=1)
+    y_rows = np.zeros((384, 256), BF16)
+    y_rows[:256, :64] = y_forward[:256]
+    y_rows[:256, 64:128] = y_forward[256:]
+    y_rows[256:320] = y_back[:, :256]
+    y_rows[320:384] = y_back[:, 256:]
+    return y_rows
+
+
+def xz_table():
+    z = np.concatenate([np.arange(0, NZ // 2, 2), np.arange(1, NZ // 2, 2)])
+    kz = np.arange(NZ)
+    x = np.arange(LX)
+    kx = np.arange(NX)
     cos, sin = phases(x, kx, NX, -1.0)
     x_forward = split_table(np.block([[cos, sin], [-sin, cos]]))
     cos, sin = phases(kx, x, NX, 1.0)
@@ -52,11 +61,6 @@
     z_forward = split_table(np.block([[cos, -sin], [sin, cos]]))
     cos, sin = phases(z, kz, NZ, 1.0)
     z_back = split_table(np.block([[cos, -sin], [sin, cos]]) / NZ)
-    y_rows = np.zeros((384, 256), BF16)
-    y_rows[:256, :64] = y_forward[:256]
-    y_rows[:256, 64:128] = y_forward[256:]
-    y_rows[256:320] = y_back[:, :256]
-    y_rows[320:384] = y_back[:, 256:]
     pieces = []
     for part in x_forward:
         pieces += [part[:, :NX], part[:, NX:]]
@@ -64,7 +68,7 @@
         pieces += [part[:NX], part[NX:]]
     pieces.append(np.concatenate(z_forward, axis=1))
     pieces.append(np.concatenate(z_back, axis=0))
-    return y_rows, np.stack(pieces)
+    return np.stack(pieces)
 
 
 def halves(values):
@@ -110,38 +114,55 @@
     earlier = grid_index((n, n), 0) < grid_index((n, n), 1)
     same = (to_column(block) == block) & earlier
     rank = jnp.sum(same.astype(jnp.int32), axis=0, keepdims=True)
-    target = jnp.where(cell_y >= 0, rank * BLOCKS + block, -1)
+    target = jnp.where(cell_y >= 0, rank * CHIPS + block, -1)
     return target, (cell_z % 2) * (NY // 2) + cell_y
 
 
-def pack_kernel(site_ref, dipoles_ref, out_ref):
+def my_core():
+    return lax.axis_index("slab") % 2
+
+
+def pack_rows(site_ref, rows, side, out_ref):
     target, place = row_targets(site_ref)
     n = target.shape[1]
     chosen = grid_index((n, n), 0) == target
     hot = chosen.astype(BF16)
-    for c in range(6):
-        v, j = divmod(c, 3)
-        rows = pick_rows(hot, dipoles_ref[c])
+    for j in range(3):
+        picked = pick_rows(hot, rows(j))
         for t in range(2):
             for p in range(2):
-                out_ref[pl.ds(13 * v + 6 * t + 2 * j + p, BLOCKS, stride=26), :] = rows[
-                    t * BLOCKS : (t + 1) * BLOCKS, p * LX : (p + 1) * LX
+                out_ref[pl.ds(6 * (2 * side + t) + 2 * j + p, CHIPS, stride=25), :] = picked[
+                    t * CHIPS : (t + 1) * CHIPS, p * LX : (p + 1) * LX
                 ]
     places = jnp.sum(jnp.where(chosen, place + 1, 0), axis=1, keepdims=True) - 1
     places = places.astype(F32)
-    lanes = grid_index((BLOCKS, LX), 1)
-    row = jnp.where(lanes == 0, places[:BLOCKS], places[BLOCKS:])
-    for v in range(2):
-        out_ref[pl.ds(13 * v + 12, BLOCKS, stride=26), :] = row
+    lanes = grid_index((CHIPS, LX), 1)
+    return jnp.where(lanes % 2 == 0, places[:CHIPS], places[CHIPS:])
+
+
+def pack_own_kernel(site_ref, dipoles_ref, out_ref):
+    core = my_core()
+    row = pack_rows(site_ref, lambda j: dipoles_ref[3 * core + j], 0, out_ref)
+    out_ref[pl.ds(24, CHIPS, stride=25), :] = row
+
+
+def pack_other_kernel(own_ref, site_ref, dipoles_ref, out_ref):
+    core = my_core()
+    out_ref[...] = own_ref[...]
+    row = pack_rows(site_ref, lambda j: dipoles_ref[3 * core + j], 1, out_ref)
+    lanes = grid_index((CHIPS, LX), 1)
+    own_row = own_ref[pl.ds(24, CHIPS, stride=25), :]
+    out_ref[pl.ds(24, CHIPS, stride=25), :] = jnp.where(lanes < 2, own_row, row)
 
 
 def slot_places(rows):
-    return jnp.concatenate([rows[:, 0:1], rows[:, 1:2]], axis=0).astype(jnp.int32)
+    return jnp.concatenate([rows[:, t : t + 1] for t in range(4)], axis=0).astype(jnp.int32)
 
 
 def y_forward_kernel(received_ref, table_ref, out_ref, places_ref):
-    slots = 2 * DEVICES
-    places = received_ref[pl.ds(12, DEVICES, stride=13), :]
+    slots = SLOTS
+    core = my_core()
+    places = received_ref[pl.ds(24, CHIPS, stride=25), :]
     places_ref[...] = places
     column = slot_places(places)
     diagonal = grid_index((slots, slots), 0) == grid_index((slots, slots), 1)
@@ -152,7 +173,7 @@
     lefts = []
     for part in range(2):
         chooser = jnp.concatenate([none, hot] if part else [hot, none], axis=0)
-        table = dot(table_ref[:256, :128], chooser).astype(BF16)
+        table = dot(table_ref[core, :256, :128], chooser).astype(BF16)
         cos = table[:128]
         sin = table[128:]
         rows = []
@@ -166,8 +187,8 @@
     for j in range(3):
         pieces = []
         for p in range(2):
-            for t in range(2):
-                pieces.append(received_ref[pl.ds(6 * t + 2 * j + p, DEVICES, stride=13), :])
+            for t in range(4):
+                pieces.append(received_ref[pl.ds(6 * t + 2 * j + p, CHIPS, stride=25), :])
         rights.append(jnp.concatenate(pieces, axis=0))
     right = halves(jnp.concatenate(rights, axis=1))
     result = dot_split(lefts, right)
@@ -182,9 +203,10 @@
 SYMMETRIC = ((0, 1, 2), (1, 3, 4), (2, 4, 5))
 
 
-def middle_kernel(received_ref, green_ref, table_ref, out_ref):
+def middle_kernel(received_ref, own_green_ref, other_green_ref, table_ref, out_ref):
     for g in range(4):
         ky = g % 2
+        green_ref = own_green_ref if g < 2 else other_green_ref
         base = 12 * g
         rows = []
         for j in range(3):
@@ -193,7 +215,7 @@
                 lanes.append(
                     jnp.concatenate(
                         [
-                            received_ref[pl.ds(base + 6 * zp + 2 * j + p, BLOCKS, stride=48), :]
+                            received_ref[pl.ds(base + 6 * zp + 2 * j + p, CHIPS, stride=48), :]
                             for zp in range(2)
                         ],
                         axis=0,
@@ -243,20 +265,21 @@
         for j in range(3):
             for p in range(2):
                 for zp in range(2):
-                    first = 64 * j + BLOCKS * zp
-                    out_ref[pl.ds(base + 6 * zp + 2 * j + p, BLOCKS, stride=48), :] = lines[
-                        first : first + BLOCKS, p * LX : (p + 1) * LX
+                    first = 64 * j + CHIPS * zp
+                    out_ref[pl.ds(base + 6 * zp + 2 * j + p, CHIPS, stride=48), :] = lines[
+                        first : first + CHIPS, p * LX : (p + 1) * LX
                     ]
 
 
 def y_back_kernel(received_ref, places_ref, table_ref, out_ref):
-    slots = 2 * DEVICES
+    slots = SLOTS
+    core = my_core()
     column = slot_places(places_ref[...])
     y = grid_index((slots, NY // 2), 1)
     hot = jnp.concatenate([(y == column).astype(BF16), (y + NY // 2 == column).astype(BF16)], axis=0)
     lefts = []
     for part in range(2):
-        table = dot(hot, table_ref[256 + 64 * part : 320 + 64 * part, :]).astype(BF16)
+        table = dot(hot, table_ref[core, 256 + 64 * part : 320 + 64 * part, :]).astype(BF16)
         cos = table[:, :128]
         sin = table[:, 128:]
         c0, c1, s0, s1 = cos[:slots], cos[slots:], sin[:slots], sin[slots:]
@@ -279,15 +302,15 @@
     right = halves(jnp.concatenate(rights, axis=1))
     result = dot_split(lefts, right)
     for p in range(2):
-        for t in range(2):
+        for t in range(4):
             for j in range(3):
-                first = p * slots + t * DEVICES
-                out_ref[pl.ds(6 * t + 2 * j + p, DEVICES, stride=12), :] = result[
-                    first : first + DEVICES, j * 128 : (j + 1) * 128
+                first = p * slots + t * CHIPS
+                out_ref[pl.ds(6 * t + 2 * j + p, CHIPS, stride=24), :] = result[
+                    first : first + CHIPS, j * 128 : (j + 1) * 128
                 ]
 
 
-def finish_kernel(received_ref, site_ref, dipoles_ref, alpha_ref, out_ref):
+def finish_rows(received_ref, side, site_ref, dipoles_ref, alpha_ref, out_ref):
     target, _ = row_targets(site_ref)
     n = target.shape[1]
     target = to_column(target)
@@ -295,48 +318,81 @@
     live = target >= 0
     alpha_re = alpha_ref[:, :LX]
     alpha_im = alpha_ref[:, LX:]
-    for c in range(6):
-        v, j = divmod(c, 3)
+    core = my_core()
+    for j in range(3):
         lanes = []
         for p in range(2):
             lanes.append(
                 jnp.concatenate(
                     [
-                        received_ref[pl.ds(12 * v + 6 * t + 2 * j + p, BLOCKS, stride=24), :]
+                        received_ref[pl.ds(6 * (2 * side + t) + 2 * j + p, CHIPS, stride=24), :]
                         for t in range(2)
                     ],
                     axis=0,
                 )
             )
         rows = pick_rows(hot, jnp.concatenate(lanes, axis=1))
+        c = 3 * (core if side == 0 else 1 - core) + j
         dip_re = dipoles_ref[c, :, :LX]
         dip_im = dipoles_ref[c, :, LX:]
-        out_ref[c, :, :LX] = jnp.where(live, alpha_re * dip_re - alpha_im * dip_im - rows[:, :LX], 0.0)
-        out_ref[c, :, LX:] = jnp.where(live, alpha_re * dip_im + alpha_im * dip_re - rows[:, LX:], 0.0)
-
-
-def call(kernel, shape, *operands, megabytes, flops=0, **more):
+        out_ref[j, :, :LX] = jnp.where(live, alpha_re * dip_re - alpha_im * dip_im - rows[:, :LX], 0.0)
+        out_ref[j, :, LX:] = jnp.where(live, alpha_re * dip_im + alpha_im * dip_re - rows[:, LX:], 0.0)
+
+
+def finish_own_kernel(received_ref, site_ref, dipoles_ref, alpha_ref, out_hbm, rows_ref, done):
+    finish_rows(received_ref, 0, site_ref, dipoles_ref, alpha_ref, rows_ref)
+    copy = pltpu.make_async_copy(rows_ref, out_hbm.at[pl.ds(3 * my_core(), 3)], done)
+    copy.start()
+    copy.wait()
+
+
+def finish_other_kernel(received_ref, site_ref, dipoles_ref, alpha_ref, own_hbm, out_hbm, rows_ref, done):
+    finish_rows(received_ref, 1, site_ref, dipoles_ref, alpha_ref, rows_ref)
+    copy = pltpu.make_async_copy(rows_ref, out_hbm.at[pl.ds(3 - 3 * my_core(), 3)], done)
+    copy.start()
+    copy.wait()
+
+
+def call(kernel, shape, *operands, megabytes, mflops=200, **more):
     whole = pl.BlockSpec(memory_space=pltpu.VMEM)
     options = dict(
         out_shape=shape and jax.ShapeDtypeStruct(shape, F32),
         in_specs=[whole] * len(operands),
         out_specs=whole,
         compiler_params=pltpu.CompilerParams(vmem_limit_bytes=megabytes * 1024 * 1024),
-        cost_estimate=pl.CostEstimate(flops=2000000000, bytes_accessed=20000000, transcendentals=0),
+        cost_estimate=pl.CostEstimate(
+            flops=mflops * 1000000, bytes_accessed=2000000, transcendentals=0
+        ),
         interpret=INTERPRET,
     )
     return pl.pallas_call(kernel, **{**options, **more})(*operands)
 
 
 def exchange(rows):
-    packed = rows.reshape(DEVICES, 1, rows.shape[0] // DEVICES * rows.shape[1])
-    moved = lax.all_to_all(packed, "slab", split_axis=0, concat_axis=0, tiled=True)
+    packed = rows.reshape(CHIPS, 1, rows.shape[0] // CHIPS * rows.shape[1])
+    groups = [[2 * chip + core for chip in range(CHIPS)] for core in range(2)]
+    moved = lax.all_to_all(
+        packed, "slab", split_axis=0, concat_axis=0, tiled=True, axis_index_groups=groups
+    )
     return moved.reshape(rows.shape)
 
 
+def swap(rows):
+    return lax.ppermute(rows, "slab", [(d, d ^ 1) for d in range(2 * CHIPS)])
+
+
 def body(dipoles, inv_alpha, row_site, green):
-    y_table, table = tables()
-    packed = call(pack_kernel, (13 * DEVICES, LX), row_site, dipoles, megabytes=4)
+    y_table = np.stack([y_tables(core) for core in range(2)])
+    table = xz_table()
+    other_dipoles = swap(dipoles)
+    other_site = swap(row_site)
+    green_rows = green.reshape(6, NZ, 2, 4, LX).transpose(0, 1, 3, 2, 4).reshape(48 * NZ, LX)
+    whole = pl.BlockSpec(memory_space=pltpu.VMEM)
+    hbm = pl.BlockSpec(memory_space=pltpu.HBM)
+    own_packed = call(pack_own_kernel, (25 * CHIPS, LX), row_site, dipoles, megabytes=4, mflops=2000)
+    packed = call(
+        pack_other_kernel, (25 * CHIPS, LX), own_packed, other_site, other_dipoles, megabytes=4, mflops=2000
+    )
     first = exchange(packed)
     planes, places = call(
         y_forward_kernel,
@@ -344,19 +400,41 @@
         first,
         y_table,
         megabytes=8,
+        mflops=1000,
         out_shape=(
-            jax.ShapeDtypeStruct((24 * DEVICES, LX), F32),
-            jax.ShapeDtypeStruct((DEVICES, LX), F32),
+            jax.ShapeDtypeStruct((48 * CHIPS, LX), F32),
+            jax.ShapeDtypeStruct((CHIPS, LX), F32),
         ),
         out_specs=(pl.BlockSpec(memory_space=pltpu.VMEM), pl.BlockSpec(memory_space=pltpu.VMEM)),
     )
+    planes, green_rows = lax.optimization_barrier((planes, green_rows))
+    other_green = swap(green_rows)
     pencils = exchange(planes)
-    green_rows = green.reshape(6, NZ, 2, 4, LX).transpose(0, 1, 3, 2, 4).reshape(48 * NZ, LX)
-    images = call(middle_kernel, (24 * DEVICES, LX), pencils, green_rows, table, megabytes=16)
+    images = call(
+        middle_kernel, (48 * CHIPS, LX), pencils, green_rows, other_green, table, megabytes=16, mflops=2000
+    )
     planes = exchange(images)
-    rows = call(y_back_kernel, (12 * DEVICES, LX), planes, places, y_table, megabytes=8)
+    rows = call(y_back_kernel, (24 * CHIPS, LX), planes, places, y_table, megabytes=8)
     returned = exchange(rows)
-    return call(finish_kernel, dipoles.shape, returned, row_site, dipoles, inv_alpha, megabytes=4)
+    other_returned = swap(returned)
+    last = dict(
+        megabytes=4,
+        out_specs=hbm,
+        scratch_shapes=[pltpu.VMEM((3,) + dipoles.shape[1:], F32), pltpu.SemaphoreType.DMA],
+    )
+    own = call(finish_own_kernel, dipoles.shape, returned, row_site, dipoles, inv_alpha, **last)
+    return call(
+        finish_other_kernel,
+        dipoles.shape,
+        other_returned,
+        row_site,
+        dipoles,
+        inv_alpha,
+        own,
+        in_specs=[whole] * 4 + [hbm],
+        input_output_aliases={4: 0},
+        **last,
+    )
 
 
 def solution(mesh):

time: 119 us -> 117 us (0.983)
  blocking collectives: 107 us -> 93.7 us
  starting transfers between devices: 0 us -> 9.38 us
  Pallas kernels: 10.2 us -> 11.4 us
    all_to_all x4, blocking collectives: 107 us -> 93.7 us  [exchange(): lax.all_to_all(packed, 'slab', split_axis=0, concat_axis=0, tiled=True, a...]
    ppermute x0 -> x4, starting transfers between devices: none -> 9.38 us  [swap(): return lax.ppermute(rows, 'slab', [(d, d ^ 1) for d in range(2 * CHIPS)])]
    pallas_call x5 -> x7, Pallas kernels: 10.2 us -> 11.4 us  [call(): return pl.pallas_call(kernel, **{**options, **more})(*operands)]
  transfers between devices with their start and end apart: 0 -> 4, of which waited for: 0 -> 1; matrix products, arithmetic and copies ran while one was open for 0% -> 0% of each run, Pallas kernels for 0% -> 1%
where the time goes in v3:
time: 117 us
  blocking collectives  93.7 us (80%)
  Pallas kernels  11.4 us (10%)
  starting transfers between devices  9.38 us (8%)
  local copies, waits for them, and re-layouts  1.71 us (1%)
    all_to_all x4, blocking collectives, exchange(): lax.all_to_all(packed, 'slab', split_axis=0, concat_axis=0, tiled=True, a...  93.7 us
    pallas_call x7, Pallas kernels, call(): return pl.pallas_call(kernel, **{**options, **more})(*operands)  11.4 us
    ppermute x4, starting transfers between devices, swap(): return lax.ppermute(rows, 'slab', [(d, d ^ 1) for d in range(2 * CHIPS)])  9.38 us
  transfers between devices with their start and end apart: 4, of which 1 were waited for; matrix products, arithmetic and copies ran while one was open for 0% of the time, Pallas kernels for 1%

profile of v3, /device:TPU:1, one launch (start us, length us, event | category | flops | bytes accessed | tf_op | source)
XLA Modules:
  0.0 116.6 jit_solution(8374388451672172357)
XLA Ops:
  0.0 3.2 %collective-permute-start.1 = (f32[6,64,256]{2,1,0:T(8,128)}, f32[6,64,256]{2,1,0:T(8,128)S(1)}, u32[]{:S(2)}, u32[]{:S(2)}) collective-permute-start(f32[6,64,256]{2,1,0:T(8,128)} %dipoles_ref.5), channel_id=1, source_target_pairs={{0,4},{4,0},{8,12},{12,8},{16,20},{20,16},{24,28},{28,24},{32,36},... | collective-permute-start | bytes 1179656 | tf_op jit(solution)/shard_map/ppermute | solution.py:381
  3.2 0.0 collective-permute-start
  3.2 1.0 copy-done.1
  4.2 0.7 copy-done.6
  4.9 0.3 shard_map.64.own_ref
  5.2 0.0 copy-start.4
  5.2 0.0 collective-permute-done.site_ref
  5.2 0.0 collective-permute-done.1.dipoles_ref
  5.2 0.3 shard_map.65
  5.6 0.0 copy-start
  5.6 0.0 copy-start.3
  5.6 23.5 %all_to_all.20 = f32[32,1,3200]{2,1,0:T(1,128)S(1)} all-to-all(f32[32,1,3200]{2,1,0:T(1,128)S(1)} %bitcast.22), channel_id=1, replica_groups={{0,8,16,24,32,40,48,56,64,72,80,88,96,104,112,120,128,136,144,152,160,1..., dimensions={0} | all-to-all | bytes 819200 | tf_op jit(solution)/shard_map/all_to_all | solution.py:374
  29.1 0.0 copy-done.4
  29.1 0.9 shard_map.66
  30.0 0.0 copy-done
  30.0 2.5 %collective-permute-start.2 = (f32[6144,128]{1,0:T(8,128)S(1)}, f32[6144,128]{1,0:T(8,128)S(1)}, u32[]{:S(2)}, u32[]{:S(2)}) collective-permute-start(f32[6144,128]{1,0:T(8,128)S(1)} %bitcast.15), channel_id=1, source_target_pairs={{0,4},{4,0},{8,12},{12,8},{16,20},{20,16},{24,28},{28,24},{32,36},... | collective-permute-start | bytes 9437192 | tf_op jit(solution)/shard_map/ppermute | solution.py:381
  32.5 25.9 %all_to_all.21 = f32[32,1,6144]{2,1,0:T(1,128)S(1)} all-to-all(f32[32,1,6144]{2,1,0:T(1,128)S(1)} %bitcast.21), channel_id=1, replica_groups={{0,8,16,24,32,40,48,56,64,72,80,88,96,104,112,120,128,136,144,152,160,1..., dimensions={0} | all-to-all | bytes 1572864 | tf_op jit(solution)/shard_map/all_to_all | solution.py:374
  58.5 0.0 collective-permute-done.2.other_green_ref
  58.5 0.0 copy-done.3
  58.5 6.8 %shard_map.67 = f32[1536,128]{1,0:T(8,128)S(1)} custom-call(f32[1536,128]{1,0:T(8,128)S(1)} %bitcast.13, f32[6144,128]{1,0:T(8,128)S(1)} %bitcast.16, f32[6144,128]{1,0:T(8,128)S(1)} %collective-permute-done.2.other_green_ref, bf16[10,256,256]{2,1,0:T(8,128)(2,1)S(1)} %copy-done.3), custom_call_target="tpu_custom_call" | custom-call | flops 2000000000 | bytes 2000000 | tf_op jit(solution)/shard_map/pallas_call | solution.py:368
  65.3 0.0 copy-start.2
  65.3 0.0 copy-start.5
  65.3 0.0 copy-start.7
  65.3 25.7 %all_to_all.22 = f32[32,1,6144]{2,1,0:T(1,128)S(1)} all-to-all(f32[32,1,6144]{2,1,0:T(1,128)S(1)} %bitcast.14), channel_id=1, replica_groups={{0,8,16,24,32,40,48,56,64,72,80,88,96,104,112,120,128,136,144,152,160,1..., dimensions={0} | all-to-all | bytes 1572864 | tf_op jit(solution)/shard_map/all_to_all | solution.py:374
  91.0 0.9 shard_map.68
  91.9 18.6 %all_to_all.23 = f32[32,1,3072]{2,1,0:T(1,128)S(1)} all-to-all(f32[32,1,3072]{2,1,0:T(1,128)S(1)} %bitcast.20), channel_id=1, replica_groups={{0,8,16,24,32,40,48,56,64,72,80,88,96,104,112,120,128,136,144,152,160,1..., dimensions={0} | all-to-all | bytes 786432 | tf_op jit(solution)/shard_map/all_to_all | solution.py:374
  110.5 3.6 %collective-permute-start.3 = (f32[768,128]{1,0:T(8,128)S(1)}, f32[768,128]{1,0:T(8,128)S(1)}, u32[]{:S(2)}, u32[]{:S(2)}) collective-permute-start(f32[768,128]{1,0:T(8,128)S(1)} %bitcast.18), channel_id=1, source_target_pairs={{0,4},{4,0},{8,12},{12,8},{16,20},{20,16},{24,28},{28,24},{32,36},... | collective-permute-start | bytes 1179656 | tf_op jit(solution)/shard_map/ppermute | solution.py:381
  114.2 0.0 copy-done.2
  114.2 0.0 copy-done.5
  114.2 1.1 shard_map.69.own_hbm
  115.3 0.2 collective-permute-done.3.received_ref
  115.5 1.1 shard_map.70
  (3 shorter events, 0.0 us)
Async XLA Ops:
  0.0 5.2 %collective-permute-start.1 = (f32[6,64,256]{2,1,0:T(8,128)}, f32[6,64,256]{2,1,0:T(8,128)S(1)}, u32[]{:S(2)}, u32[]{:S(2)}) collective-permute-start(f32[6,64,256]{2,1,0:T(8,128)} %dipoles_ref.5), channel_id=1, source_target_pairs={{0,4},{4,0},{8,12},{12,8},{16,20},{20,16},{24,28},{28,24},{32,36},... | collective-permute-start | bytes 1179656 | tf_op jit(solution)/shard_map/ppermute | solution.py:381
  3.2 2.0 %collective-permute-start = (s32[2,64]{1,0:T(2,128)}, s32[2,64]{1,0:T(2,128)S(1)}, u32[]{:S(2)}, u32[]{:S(2)}) collective-permute-start(s32[2,64]{1,0:T(2,128)} %site_ref.5), channel_id=1, source_target_pairs={{0,4},{4,0},{8,12},{12,8},{16,20},{20,16},{24,28},{28,24},{32,36},... | collective-permute-start | bytes 1544 | tf_op jit(solution)/shard_map/ppermute | solution.py:381
  3.2 1.0 copy-start.1
  4.2 0.7 copy-start.6
  5.2 23.9 %copy-start.4 = (bf16[2,384,256]{2,1,0:T(8,128)(2,1)S(1)}, bf16[2,384,256]{2,1,0:T(8,128)(2,1)}, u32[]{:S(2)}) copy-start(bf16[2,384,256]{2,1,0:T(8,128)(2,1)} %constant.4.clone.table_ref) | copy-start | bytes 1179652
  5.6 24.4 %copy-start = (f32[6,128,2,512]{3,2,1,0:T(2,128)S(1)}, f32[6,128,2,512]{3,2,1,0:T(2,128)}, u32[]{:S(2)}) copy-start(f32[6,128,2,512]{3,2,1,0:T(2,128)} %param.9) | copy-start | bytes 9437188
  5.6 52.9 %copy-start.3 = (bf16[10,256,256]{2,1,0:T(8,128)(2,1)S(1)}, bf16[10,256,256]{2,1,0:T(8,128)(2,1)}, u32[]{:S(2)}) copy-start(bf16[10,256,256]{2,1,0:T(8,128)(2,1)} %constant.5.clone.table_ref) | copy-start | bytes 3932164
  30.0 28.5 %collective-permute-start.2 = (f32[6144,128]{1,0:T(8,128)S(1)}, f32[6144,128]{1,0:T(8,128)S(1)}, u32[]{:S(2)}, u32[]{:S(2)}) collective-permute-start(f32[6144,128]{1,0:T(8,128)S(1)} %bitcast.15), channel_id=1, source_target_pairs={{0,4},{4,0},{8,12},{12,8},{16,20},{20,16},{24,28},{28,24},{32,36},... | collective-permute-start | bytes 9437192 | tf_op jit(solution)/shard_map/ppermute | solution.py:381
  65.3 48.9 %copy-start.2 = (f32[6,64,256]{2,1,0:T(8,128)S(1)}, f32[6,64,256]{2,1,0:T(8,128)}, u32[]{:S(2)}) copy-start(f32[6,64,256]{2,1,0:T(8,128)} %dipoles_ref.5) | copy-start | bytes 1179652
  65.3 48.9 %copy-start.5 = (f32[64,256]{1,0:T(8,128)S(1)}, f32[64,256]{1,0:T(8,128)}, u32[]{:S(2)}) copy-start(f32[64,256]{1,0:T(8,128)} %alpha_ref.3) | copy-start | bytes 196612
  65.3 48.9 %copy-start.7 = (s32[2,64]{1,0:T(2,128)S(1)}, s32[2,64]{1,0:T(2,128)}, u32[]{:S(2)}) copy-start(s32[2,64]{1,0:T(2,128)} %site_ref.5) | copy-start | bytes 1540
  110.5 5.0 %collective-permute-start.3 = (f32[768,128]{1,0:T(8,128)S(1)}, f32[768,128]{1,0:T(8,128)S(1)}, u32[]{:S(2)}, u32[]{:S(2)}) collective-permute-start(f32[768,128]{1,0:T(8,128)S(1)} %bitcast.18), channel_id=1, source_target_pairs={{0,4},{4,0},{8,12},{12,8},{16,20},{20,16},{24,28},{28,24},{32,36},... | collective-permute-start | bytes 1179656 | tf_op jit(solution)/shard_map/ppermute | solution.py:381
